TPU v7x, 128 devices: a whole 4x4x4 slice. The times are simulated.
128 devices in a mesh: slc: 64 (over x_hi, y, z, core), col: 2 (over x_lo).
Axes of the slice: x: 4 (x_hi: 2, x_lo: 2; x = x_hi * 2 + x_lo), y: 4, z: 4, core: 2. Of those that a mesh axis runs over, the one named last changes fastest.
Arguments:
- basis: bfloat16 [64, 2, 1152, 3456], P('slc', None, None, 'col'), may hold values from -6 to 6
- picks: int32 [64, 608], P('slc', 'col'), may hold values from 0 to 1727, as said below
- coil_maps: bfloat16 [128, 64, 2, 32, 128], P('slc'), may hold values from -6 to 6
Outputs:
- mapped: bfloat16 [128, 64, 2, 32, 128], P('slc', None, None, 'col')
Inputs may be any that keep to these rules, and one draw needn't show every extreme that they name: `picks`: for each slice, the entries in each of the 2 blocks of 304 positions are distinct offsets within the corresponding block of 1728 calibration windows.
All inputs are finite; a program needn't handle non-finite values.
Results may differ from a plain program's by a relative error of at most 0.0049.
Values may be sent and summed in bfloat16 or wider, within the bound.
No kernel may reach another device: no remote copies, remote signals or barrier semaphores. Data moves between devices by JAX's collectives and lax.ppermute only.
A program may use at most 448 MiB of HBM per device.

v0:
```python
import math

import jax
import jax.numpy as jnp
import numpy as np
from jax import lax
from jax.experimental import pallas as pl
from jax.experimental.pallas import tpu as pltpu
from jax.sharding import PartitionSpec as P

COILS = 32
KSIZE = 6
RANK = 608
IMG = 128
SPAN = 2 * KSIZE - 1
LANES = 128
AROWS = KSIZE * COILS
WIDE = 384
SBLOCK = 8


def gram_kernel(picks_ref, basis_ref, keep_ref, send_ref, buffer, onehot, rows, left, right, sems):
    windows = basis_ref.shape[1]
    width = basis_ref.shape[2]
    used = picks_ref.shape[1]
    cuts = [(0, 512), (512, width - 512)]
    copies = [
        pltpu.make_async_copy(
            basis_ref.at[part, :, pl.ds(first, size)],
            buffer.at[part, :, pl.ds(first, size)],
            sems.at[part, index],
        )
        for part in range(2)
        for index, (first, size) in enumerate(cuts)
    ]
    for copy in copies:
        copy.start()

    wanted = jnp.concatenate(
        [picks_ref[...], jnp.full((1, WIDE - used), -1, jnp.int32)], axis=1
    )
    wanted = jnp.broadcast_to(wanted, (LANES, WIDE)).T[:used]
    lane = lax.broadcasted_iota(jnp.int32, (used, LANES), 1)
    for first in range(0, windows, LANES):
        size = min(LANES, windows - first)
        match = jnp.where(wanted == lane + first, 1.0, 0.0).astype(jnp.bfloat16)
        onehot[:, first : first + size] = match[:, :size]
    right[:, AROWS:, :] = jnp.zeros((2, right.shape[1] - AROWS, right.shape[2]), jnp.bfloat16)

    for part in range(2):
        for index, (first, size) in enumerate(cuts):
            copies[part * len(cuts) + index].wait()
            picked = jnp.dot(
                onehot[...],
                buffer[part, :, first : first + size],
                preferred_element_type=jnp.float32,
            )
            picked = jnp.concatenate([picked, jnp.zeros((WIDE - used, size), jnp.float32)], axis=0)
            for tile in range(WIDE // LANES):
                rows[part, tile, first : first + size] = picked[
                    tile * LANES : (tile + 1) * LANES
                ].T
        for a in range(KSIZE):
            for b in range(KSIZE):
                for tile in range(WIDE // LANES):
                    block = rows[
                        part, tile, pl.ds(a * KSIZE + b, COILS, stride=KSIZE * KSIZE), :
                    ].astype(jnp.bfloat16)
                    row = slice(a * COILS, (a + 1) * COILS)
                    spot = slice(b * WIDE + tile * LANES, b * WIDE + (tile + 1) * LANES)
                    left[part, row, spot] = block
                    right[part, row, spot] = block

    def against(q, part):
        depth = (KSIZE - q) * WIDE
        lhs = left[:, :, :depth].reshape(2 * AROWS, depth)
        return lax.dot_general(
            lhs,
            right[part, :, q * WIDE :],
            (((1,), (1,)), ((), ())),
            preferred_element_type=jnp.float32,
        )

    pad = jnp.zeros((COILS, WIDE - right.shape[1]), jnp.float32)
    for q in range(KSIZE):
        with_real = against(q, 0)
        with_imag = against(q, 1)
        pair = (
            with_real[:AROWS] + with_imag[AROWS:],
            with_real[AROWS:] - with_imag[:AROWS],
        )
        for part in range(2):
            total = None
            for a in range(KSIZE):
                block = jnp.concatenate([pair[part][a * COILS : (a + 1) * COILS], pad], axis=1)
                shift = (KSIZE - 1 - a) * COILS
                moved = pltpu.roll(block, shift, 1) if shift else block
                total = moved if total is None else total + moved
            keep_ref[q, part] = total
            send_ref[q, part] = total.astype(jnp.bfloat16)


def partial_kernels(basis, picks):
    turned = pltpu.with_memory_space_constraint(jnp.transpose(basis, (0, 2, 1)), pltpu.HBM)
    parts, windows, rows = turned.shape
    used = picks.shape[1]
    return pl.pallas_call(
        gram_kernel,
        in_specs=[
            pl.BlockSpec(memory_space=pltpu.VMEM),
            pl.BlockSpec(memory_space=pltpu.HBM),
        ],
        out_specs=[pl.BlockSpec(memory_space=pltpu.VMEM)] * 2,
        out_shape=[
            jax.ShapeDtypeStruct((KSIZE, 2, COILS, WIDE), jnp.float32),
            jax.ShapeDtypeStruct((KSIZE, 2, COILS, WIDE), jnp.bfloat16),
        ],
        scratch_shapes=[
            pltpu.VMEM((parts, windows, rows), jnp.bfloat16),
            pltpu.VMEM((used, windows), jnp.bfloat16),
            pltpu.VMEM((parts, WIDE // LANES, rows, LANES), jnp.float32),
            pltpu.VMEM((2, AROWS, KSIZE * WIDE), jnp.bfloat16),
            pltpu.VMEM((2, 256, KSIZE * WIDE), jnp.bfloat16),
            pltpu.SemaphoreType.DMA((parts, 2)),
        ],
        compiler_params=pltpu.CompilerParams(vmem_limit_bytes=24 * 2**20),
        name="partial_kernels",
    )(picks, turned)


def transform_table():
    half = IMG // 4
    table = np.zeros((half, 16, LANES), np.float32)
    for first in range(half):
        for q in range(1, KSIZE):
            lanes_y = np.repeat(2 * first + np.arange(2), LANES // 2)
            angle = 2.0 * math.pi * ((q * lanes_y) % IMG) / IMG
            table[first, q - 1] = np.cos(angle)
            table[first, KSIZE - 2 + q] = np.sin(angle)
    return table


def transform_kernel(half_ref, keep_ref, got_ref, table_ref, out_ref, whole, turned, terms):
    coil_share = COILS // 2

    def build():
        factor = 1.0 / (2.0 * RANK * KSIZE * KSIZE)
        own = pl.multiple_of(half_ref[0] * coil_share, coil_share)
        lane = lax.broadcasted_iota(jnp.int32, (coil_share, LANES), 1)
        group = lane // COILS
        even_slot = group % 2 == 0
        low_half = lane < LANES // 2
        swap_sign = jnp.where(even_slot, -1.0, 1.0)
        centre = KSIZE - 1

        def forward(q):
            found = []
            for tile in range(WIDE // LANES):
                lanes = slice(tile * LANES, (tile + 1) * LANES)
                real = whole[q, 0, pl.ds(own, coil_share), lanes]
                imag = whole[q, 1, pl.ds(own, coil_share), lanes]
                first = jnp.where(even_slot, real, pltpu.roll(imag, COILS, 1))
                second = jnp.where(even_slot, pltpu.roll(real, LANES - COILS, 1), imag)
                first_turned = pltpu.roll(first, LANES // 2, 1)
                second_turned = pltpu.roll(second, LANES // 2, 1)
                found += [
                    jnp.where(low_half, first, first_turned),
                    jnp.where(low_half, second, second_turned),
                    jnp.where(low_half, first_turned, first),
                    jnp.where(low_half, second_turned, second),
                ]
            return found[:SPAN]

        def place(index, values):
            terms[index, :coil_share] = values[centre]
            for offset in range(1, KSIZE):
                upper = values[centre + offset]
                lower = values[centre - offset]
                even = offset * coil_share
                odd = (offset + KSIZE - 1) * coil_share
                terms[index, even : even + coil_share] = upper + lower
                terms[index, odd : odd + coil_share] = upper - lower

        def one_shift(q, carry):
            real = (keep_ref[q, 0] + got_ref[q, 0].astype(jnp.float32)) * factor
            imag = (keep_ref[q, 1] + got_ref[q, 1].astype(jnp.float32)) * factor
            whole[q, 0] = real
            whole[q, 1] = imag
            turned[...] = jnp.concatenate([real, -imag, real, -imag], axis=0).T
            ahead = forward(q)
            sums = []
            gaps = []
            for p in range(SPAN):
                row = pl.multiple_of((SPAN - 1 - p) * COILS + own, coil_share)
                behind = turned[pl.ds(row, coil_share), :]
                sums.append(ahead[p] + behind)
                gaps.append(pltpu.roll(ahead[p] - behind, COILS, 1) * swap_sign)
            place(q, sums)
            place(KSIZE - 1 + q, gaps)
            return carry

        for part in range(2):
            whole[0, part] = (keep_ref[0, part] + got_ref[0, part].astype(jnp.float32)) * factor
        place(0, forward(0))
        lax.fori_loop(1, KSIZE, one_shift, 0)

    build()
    blocks = table_ref.shape[0]
    group_size = 2

    def one(step, carry):
        places = [step * group_size + extra for extra in range(group_size)]
        weights = [
            [
                jnp.broadcast_to(table_ref[place, index : index + 1, :], (8, LANES))
                for index in range(2 * KSIZE - 2)
            ]
            for place in places
        ]
        for block in range(SPAN):
            made = [[] for _ in places]
            for sub in range(2):
                rows = slice(block * coil_share + sub * 8, block * coil_share + sub * 8 + 8)
                cells = [terms[index, rows] for index in range(2 * KSIZE - 1)]
                for extra in range(group_size):
                    even = cells[0]
                    odd = None
                    for q in range(1, KSIZE):
                        piece = (
                            cells[q] * weights[extra][q - 1]
                            + cells[KSIZE - 1 + q] * weights[extra][KSIZE - 2 + q]
                        )
                        if q % 2 == 0:
                            even = even + piece
                        else:
                            odd = piece if odd is None else odd + piece
                    made[extra].append((even + odd, even - odd))
            rows = slice(block * coil_share, (block + 1) * coil_share)
            for extra, place in enumerate(places):
                for sign in range(2):
                    whole_rows = jnp.concatenate([half[sign] for half in made[extra]], axis=0)
                    out_ref[place + sign * blocks, rows, :] = whole_rows.astype(jnp.bfloat16)
        return carry

    lax.fori_loop(0, blocks // group_size, one, 0)


def column_rows(half, keep, got):
    blocks = IMG // 2
    rows = SPAN * COILS // 2
    return pl.pallas_call(
        transform_kernel,
        in_specs=[pl.BlockSpec(memory_space=pltpu.SMEM)]
        + [pl.BlockSpec(memory_space=pltpu.VMEM)] * 3,
        out_specs=pl.BlockSpec(memory_space=pltpu.VMEM),
        scratch_shapes=[
            pltpu.VMEM((KSIZE, 2, COILS, WIDE), jnp.float32),
            pltpu.VMEM((WIDE, LANES), jnp.float32),
            pltpu.VMEM((2 * KSIZE - 1, rows + 8, LANES), jnp.float32),
        ],
        out_shape=jax.ShapeDtypeStruct((blocks, rows, LANES), jnp.bfloat16),
        compiler_params=pltpu.CompilerParams(vmem_limit_bytes=16 * 2**20),
        name="column_rows",
    )(half, keep, got, jnp.asarray(transform_table()))


def phase_table():
    table = np.zeros((16, IMG), np.float32)
    for p in range(1, KSIZE):
        angle = 2.0 * math.pi * ((p * np.arange(IMG)) % IMG) / IMG
        table[p - 1] = np.cos(angle)
        table[KSIZE - 2 + p] = np.sin(angle)
    return table


def apply_kernel(rows_ref, maps_ref, table_ref, out_ref, result, sems):
    coil_share = COILS // 2
    slices = rows_ref.shape[0]
    waves = [
        jnp.broadcast_to(table_ref[index : index + 1, :], (coil_share, IMG))
        for index in range(2 * KSIZE - 2)
    ]
    blank = jnp.zeros((2 * COILS, 2 * IMG), jnp.bfloat16)

    def one(index, y):
        real = maps_ref[y, index, 0]
        imag = maps_ref[y, index, 1]
        filled = jnp.concatenate(
            [
                jnp.concatenate([real, imag], axis=1),
                jnp.concatenate([-imag, real], axis=1),
            ],
            axis=0,
        )
        halves = [filled, blank] if y == 0 else [blank, filled]
        mixed = jnp.dot(
            rows_ref[index], jnp.concatenate(halves, axis=0), preferred_element_type=jnp.float32
        )

        def piece(place, part):
            return mixed[
                place * coil_share : (place + 1) * coil_share, part * IMG : (part + 1) * IMG
            ]

        out_real = piece(0, 0)
        out_imag = piece(0, 1)
        for p in range(1, KSIZE):
            cosine = waves[p - 1]
            sine = waves[KSIZE - 2 + p]
            out_real = out_real + (piece(p, 0) * cosine - piece(KSIZE - 1 + p, 1) * sine)
            out_imag = out_imag + (piece(p, 1) * cosine + piece(KSIZE - 1 + p, 0) * sine)
        result[y, index, 0] = out_real.astype(jnp.bfloat16)
        result[y, index, 1] = out_imag.astype(jnp.bfloat16)

    def write(step, y):
        span = pl.ds(step * SBLOCK, SBLOCK)
        return pltpu.make_async_copy(result.at[y, span], out_ref.at[y, span], sems.at[step, y])

    def block(step, carry):
        for local in range(SBLOCK):
            for y in range(2):
                one(step * SBLOCK + local, y)
        for y in range(2):
            write(step, y).start()
        return carry

    steps = slices // SBLOCK
    lax.fori_loop(0, steps, block, 0)

    def finish(step, carry):
        for y in range(2):
            write(step, y).wait()
        return carry

    lax.fori_loop(0, steps, finish, 0)


def apply_rows(rows, maps):
    slices = rows.shape[0]
    width = maps.shape[0]
    shape = (width, slices, 2, COILS // 2, IMG)
    return pl.pallas_call(
        apply_kernel,
        in_specs=[pl.BlockSpec(memory_space=pltpu.VMEM)] * 3,
        out_specs=pl.BlockSpec(memory_space=pltpu.HBM),
        out_shape=jax.ShapeDtypeStruct(shape, jnp.bfloat16),
        scratch_shapes=[
            pltpu.VMEM(shape, jnp.bfloat16),
            pltpu.SemaphoreType.DMA((slices // SBLOCK, width)),
        ],
        compiler_params=pltpu.CompilerParams(vmem_limit_bytes=16 * 2**20),
        name="apply_rows",
    )(rows, maps, jnp.asarray(phase_table()))


def shards(basis, picks, coil_maps):
    half = lax.axis_index("col").astype(jnp.int32).reshape(1)
    keep, send = partial_kernels(basis[0], picks)
    got = lax.ppermute(send, "col", [(0, 1), (1, 0)])
    rows = column_rows(half, keep, got)
    rows = lax.all_to_all(rows, "slc", split_axis=0, concat_axis=0, tiled=True)
    return apply_rows(rows, coil_maps)


def solution(mesh):
    placed = (P("slc", None, None, "col"), P("slc", "col"), P("slc", None, None, None, None))
    return jax.shard_map(
        shards,
        mesh=mesh,
        in_specs=placed,
        out_specs=P("slc", None, None, "col", None),
        check_vma=False,
    )
```

profile of v0, /device:TPU:1, one launch (start us, length us, event | category | flops | bytes accessed | tf_op | source)
XLA Modules:
  0.0 79.1 jit_solution(1486570630893069168)
XLA Ops:
  0.0 0.0 copy-start.3
  0.0 0.7 copy-done.3
  0.7 0.0 copy-start.1
  0.7 9.9 %partial_kernels.1 = (f32[6,2,32,384]{3,2,1,0:T(8,128)S(1)}, bf16[6,2,32,384]{3,2,1,0:T(8,128)(2,1)S(1)}) custom-call(s32[1,304]{1,0:T(1,128)S(1)} %copy-done.3, bf16[2,1728,1152]{2,1,0:T(8,128)(2,1)} %bitcast.4), custom_call_target="tpu_custom_call" | custom-call | tf_op jit(solution)/shard_map/partial_kernels/pallas_call | solution.py:107
  10.6 2.1 %collective-permute-start = (bf16[6,2,32,384]{3,2,1,0:T(8,128)(2,1)S(1)}, bf16[6,2,32,384]{3,2,1,0:T(8,128)(2,1)S(1)}, u32[]{:S(2)}, u32[]{:S(2)}) collective-permute-start(bf16[6,2,32,384]{3,2,1,0:T(8,128)(2,1)S(1)} %get-tuple-element.8), channel_id=1, source_target_pairs={{0,1},{1,0},{2,3},{3,2},{4,5},{5,4},{6,7},{7,6},{8,9},{9,8},{10,11... | collective-permute-start | bytes 884744 | tf_op jit(solution)/shard_map/ppermute | solution.py:359
  12.7 6.3 %collective-permute-done.got_ref = bf16[6,2,32,384]{3,2,1,0:T(8,128)(2,1)S(1)} collective-permute-done((bf16[6,2,32,384]{3,2,1,0:T(8,128)(2,1)S(1)}, bf16[6,2,32,384]{3,2,1,0:T(8,128)(2,1)S(1)}, u32[]{:S(2)}, u32[]{:S(2)}) %collective-permute-start) | collective-permute-done | bytes 294944 | tf_op jit(solution)/shard_map/ppermute | solution.py:359
  19.0 0.0 copy-done.1
  19.0 3.7 %column_rows.1 = bf16[64,176,128]{2,1,0:T(8,128)(2,1)S(1)} custom-call(s32[1]{0:T(128)} %bitcast.half_ref, f32[6,2,32,384]{3,2,1,0:T(8,128)S(1)} %get-tuple-element.7.keep_ref, bf16[6,2,32,384]{3,2,1,0:T(8,128)(2,1)S(1)} %collective-permute-done.got_ref, f32[32,16,128]{2,1,0:T(8,128)S(1)} %copy-done.1), custom_call_target="tpu_custom_call" | custom-call | tf_op jit(solution)/shard_map/column_rows/pallas_call | solution.py:251
  22.7 0.0 copy-start
  22.7 0.0 copy-start.2
  22.7 51.4 %all_to_all.5.rows_ref = bf16[64,176,128]{2,1,0:T(8,128)(2,1)S(1)} all-to-all(bf16[64,176,128]{2,1,0:T(8,128)(2,1)S(1)} %column_rows.1), channel_id=1, replica_groups=mesh['slc'=64,'col'=2] {'slc'}, dimensions={0} | all-to-all | bytes 5767168 | tf_op jit(solution)/shard_map/all_to_all | solution.py:361
  74.1 0.0 copy-done
  74.1 0.0 copy-done.2
  74.1 5.0 %apply_rows.1 = bf16[2,64,2,16,128]{4,3,2,1,0:T(8,128)(2,1)} custom-call(bf16[64,176,128]{2,1,0:T(8,128)(2,1)S(1)} %all_to_all.5.rows_ref, bf16[2,64,2,32,128]{4,3,2,1,0:T(8,128)(2,1)S(1)} %copy-done, f32[16,128]{1,0:T(8,128)S(1)} %copy-done.2), custom_call_target="tpu_custom_call" | custom-call | tf_op jit(solution)/shard_map/apply_rows/pallas_call | solution.py:342
Async XLA Ops:
  0.0 0.7 copy-start.3
  0.7 18.3 %copy-start.1 = (f32[32,16,128]{2,1,0:T(8,128)S(1)}, f32[32,16,128]{2,1,0:T(8,128)}, u32[]{:S(2)}) copy-start(f32[32,16,128]{2,1,0:T(8,128)} %constant.8.clone.table_ref) | copy-start | bytes 786436
  10.6 8.4 %collective-permute-start = (bf16[6,2,32,384]{3,2,1,0:T(8,128)(2,1)S(1)}, bf16[6,2,32,384]{3,2,1,0:T(8,128)(2,1)S(1)}, u32[]{:S(2)}, u32[]{:S(2)}) collective-permute-start(bf16[6,2,32,384]{3,2,1,0:T(8,128)(2,1)S(1)} %get-tuple-element.8), channel_id=1, source_target_pairs={{0,1},{1,0},{2,3},{3,2},{4,5},{5,4},{6,7},{7,6},{8,9},{9,8},{10,11... | collective-permute-start | bytes 884744 | tf_op jit(solution)/shard_map/ppermute | solution.py:359
  22.7 51.4 %copy-start = (bf16[2,64,2,32,128]{4,3,2,1,0:T(8,128)(2,1)S(1)}, bf16[2,64,2,32,128]{4,3,2,1,0:T(8,128)(2,1)}, u32[]{:S(2)}) copy-start(bf16[2,64,2,32,128]{4,3,2,1,0:T(8,128)(2,1)} %maps_ref.1) | copy-start | bytes 6291460
  22.7 51.4 %copy-start.2 = (f32[16,128]{1,0:T(8,128)S(1)}, f32[16,128]{1,0:T(8,128)}, u32[]{:S(2)}) copy-start(f32[16,128]{1,0:T(8,128)} %constant.9.clone.table_ref) | copy-start | bytes 24580
where the time goes:
time: 79.3 us; the launch traced here: 79.1 us
  blocking collectives  51.4 us (65%)
  Pallas kernels  18.6 us (23%)
  waiting for transfers between devices  6.3 us (8%)
  starting transfers between devices  2.11 us (3%)
    all_to_all x1, blocking collectives, shards(): rows = lax.all_to_all(rows, 'slc', split_axis=0, concat_axis=0, tiled=True)  51.4 us
    pallas_call x1, Pallas kernels, partial_kernels(): pl.pallas_call(gram_kernel, in_specs=[pl.BlockSpec(memory_space=pltpu.VME...  9.87 us
    ppermute x1, waiting for transfers between devices, shards(): got = lax.ppermute(send, 'col', [(0, 1), (1, 0)])  6.3 us
    pallas_call x1, Pallas kernels, apply_rows(): pl.pallas_call(apply_kernel, in_specs=[pl.BlockSpec(memory_space=pltpu.VM...  5.03 us
    pallas_call x1, Pallas kernels, column_rows(): pl.pallas_call(transform_kernel, in_specs=[pl.BlockSpec(memory_space=pltp...  3.69 us
    ppermute x1, starting transfers between devices, shards(): got = lax.ppermute(send, 'col', [(0, 1), (1, 0)])  2.11 us
  transfers between devices with their start and end apart: 1, of which 1 were waited for; matrix products, arithmetic and copies ran while one was open for 0% of the time, Pallas kernels for 0%

commit v1 on v0

--- a/solution.py
+++ b/solution.py
@@ -16,7 +16,9 @@
 LANES = 128
 AROWS = KSIZE * COILS
 WIDE = 384
-SBLOCK = 8
+SBLOCK = 4
+PACKED = 136
+BF = jnp.bfloat16
 
 
 def gram_kernel(picks_ref, basis_ref, keep_ref, send_ref, buffer, onehot, rows, left, right, sems):
@@ -146,6 +148,7 @@
     def build():
         factor = 1.0 / (2.0 * RANK * KSIZE * KSIZE)
         own = pl.multiple_of(half_ref[0] * coil_share, coil_share)
+        other = pl.multiple_of(coil_share - half_ref[0] * coil_share, coil_share)
         lane = lax.broadcasted_iota(jnp.int32, (coil_share, LANES), 1)
         group = lane // COILS
         even_slot = group % 2 == 0
@@ -153,12 +156,20 @@
         swap_sign = jnp.where(even_slot, -1.0, 1.0)
         centre = KSIZE - 1
 
+        own_lane = lane // coil_share % 2 == 0
+        upper_half = half_ref[0] == 1
+
+        def own_first(value):
+            down = pltpu.roll(value, LANES - coil_share, 1)
+            up = pltpu.roll(value, coil_share, 1)
+            return jnp.where(upper_half, jnp.where(own_lane, down, up), value)
+
         def forward(q):
             found = []
             for tile in range(WIDE // LANES):
                 lanes = slice(tile * LANES, (tile + 1) * LANES)
-                real = whole[q, 0, pl.ds(own, coil_share), lanes]
-                imag = whole[q, 1, pl.ds(own, coil_share), lanes]
+                real = own_first(whole[q, 0, pl.ds(own, coil_share), lanes])
+                imag = own_first(whole[q, 1, pl.ds(own, coil_share), lanes])
                 first = jnp.where(even_slot, real, pltpu.roll(imag, COILS, 1))
                 second = jnp.where(even_slot, pltpu.roll(real, LANES - COILS, 1), imag)
                 first_turned = pltpu.roll(first, LANES // 2, 1)
@@ -171,22 +182,38 @@
                 ]
             return found[:SPAN]
 
+        toward_own = LANES - coil_share
+
         def place(index, values):
             terms[index, :coil_share] = values[centre]
+            gaps = []
             for offset in range(1, KSIZE):
                 upper = values[centre + offset]
                 lower = values[centre - offset]
-                even = offset * coil_share
-                odd = (offset + KSIZE - 1) * coil_share
-                terms[index, even : even + coil_share] = upper + lower
-                terms[index, odd : odd + coil_share] = upper - lower
+                row = offset * coil_share
+                terms[index, row : row + coil_share] = jnp.where(own_lane, upper, upper + lower)
+                gaps.append(upper - lower)
+            row = KSIZE * coil_share
+            for pair in range(2):
+                moved = pltpu.roll(gaps[2 * pair + 1], toward_own, 1)
+                terms[index, row : row + coil_share] = jnp.where(own_lane, moved, gaps[2 * pair])
+                row += coil_share
+            moved = pltpu.roll(gaps[4], toward_own, 1)
+            rest = coil_share // 2
+            terms[index, row : row + rest] = jnp.where(own_lane[:rest], moved[rest:], gaps[4][:rest])
 
         def one_shift(q, carry):
             real = (keep_ref[q, 0] + got_ref[q, 0].astype(jnp.float32)) * factor
             imag = (keep_ref[q, 1] + got_ref[q, 1].astype(jnp.float32)) * factor
             whole[q, 0] = real
             whole[q, 1] = imag
-            turned[...] = jnp.concatenate([real, -imag, real, -imag], axis=0).T
+            ordered = [
+                whole[q, part, pl.ds(first, coil_share), :]
+                for part in range(2)
+                for first in (own, other)
+            ]
+            ordered = [ordered[0], ordered[1], -ordered[2], -ordered[3]]
+            turned[...] = jnp.concatenate(ordered + ordered, axis=0).T
             ahead = forward(q)
             sums = []
             gaps = []
@@ -217,11 +244,11 @@
             ]
             for place in places
         ]
-        for block in range(SPAN):
+        for first in range(0, PACKED, coil_share):
             made = [[] for _ in places]
-            for sub in range(2):
-                rows = slice(block * coil_share + sub * 8, block * coil_share + sub * 8 + 8)
-                cells = [terms[index, rows] for index in range(2 * KSIZE - 1)]
+            last = min(first + coil_share, PACKED)
+            for row in range(first, last, 8):
+                cells = [terms[index, row : row + 8] for index in range(2 * KSIZE - 1)]
                 for extra in range(group_size):
                     even = cells[0]
                     odd = None
@@ -235,11 +262,10 @@
                         else:
                             odd = piece if odd is None else odd + piece
                     made[extra].append((even + odd, even - odd))
-            rows = slice(block * coil_share, (block + 1) * coil_share)
             for extra, place in enumerate(places):
                 for sign in range(2):
                     whole_rows = jnp.concatenate([half[sign] for half in made[extra]], axis=0)
-                    out_ref[place + sign * blocks, rows, :] = whole_rows.astype(jnp.bfloat16)
+                    out_ref[place + sign * blocks, first:last, :] = whole_rows.astype(jnp.bfloat16)
         return carry
 
     lax.fori_loop(0, blocks // group_size, one, 0)
@@ -247,7 +273,6 @@
 
 def column_rows(half, keep, got):
     blocks = IMG // 2
-    rows = SPAN * COILS // 2
     return pl.pallas_call(
         transform_kernel,
         in_specs=[pl.BlockSpec(memory_space=pltpu.SMEM)]
@@ -256,9 +281,9 @@
         scratch_shapes=[
             pltpu.VMEM((KSIZE, 2, COILS, WIDE), jnp.float32),
             pltpu.VMEM((WIDE, LANES), jnp.float32),
-            pltpu.VMEM((2 * KSIZE - 1, rows + 8, LANES), jnp.float32),
+            pltpu.VMEM((2 * KSIZE - 1, PACKED, LANES), jnp.float32),
         ],
-        out_shape=jax.ShapeDtypeStruct((blocks, rows, LANES), jnp.bfloat16),
+        out_shape=jax.ShapeDtypeStruct((blocks, PACKED, LANES), jnp.bfloat16),
         compiler_params=pltpu.CompilerParams(vmem_limit_bytes=16 * 2**20),
         name="column_rows",
     )(half, keep, got, jnp.asarray(transform_table()))
@@ -273,7 +298,7 @@
     return table
 
 
-def apply_kernel(rows_ref, maps_ref, table_ref, out_ref, result, sems):
+def apply_kernel(half_ref, rows_ref, maps_ref, table_ref, out_ref, result, even_rows, odd_rows, sems):
     coil_share = COILS // 2
     slices = rows_ref.shape[0]
     waves = [
@@ -281,10 +306,55 @@
         for index in range(2 * KSIZE - 2)
     ]
     blank = jnp.zeros((2 * COILS, 2 * IMG), jnp.bfloat16)
-
-    def one(index, y):
-        real = maps_ref[y, index, 0]
-        imag = maps_ref[y, index, 1]
+    own = pl.multiple_of(half_ref[0] * coil_share, coil_share)
+    other = pl.multiple_of(coil_share - half_ref[0] * coil_share, coil_share)
+    lane = lax.broadcasted_iota(jnp.int32, (coil_share, LANES), 1)
+    own_lane = lane // coil_share % 2 == 0
+    group = lane // COILS
+    groups = LANES // COILS
+    buffers = (even_rows, odd_rows)
+
+    def unpack(index, lhs, local):
+        def tile(place):
+            return rows_ref[index, place * coil_share : (place + 1) * coil_share, :]
+
+        def spread(packed):
+            return packed, pltpu.roll(packed, coil_share, 1)
+
+        first, second = spread(tile(KSIZE))
+        third, fourth = spread(tile(KSIZE + 1))
+        tail = spread(rows_ref[index, (KSIZE + 2) * coil_share :, :])
+        crossed = [first, second, third, fourth, jnp.concatenate(tail, axis=0)]
+        merged = [tile(place) for place in range(KSIZE)]
+        stacked = jnp.concatenate(merged[1:] + [jnp.zeros((3 * coil_share, LANES), BF)], axis=0).T
+        strips = []
+        for target in range(groups):
+            strip = stacked[target * COILS : target * COILS + coil_share]
+            strips.append(-strip if target % 2 else strip)
+        lhs[local, :coil_share] = merged[0]
+        for p in range(1, KSIZE):
+            mirror = None
+            for target in range(groups):
+                shift = (target * COILS - (p - 1) * coil_share) % LANES
+                moved = pltpu.roll(strips[target], shift, 1) if shift else strips[target]
+                mirror = moved if mirror is None else jnp.where(group == target, moved, mirror)
+            row = p * coil_share
+            lhs[local, row : row + coil_share] = jnp.where(
+                own_lane, merged[p] + mirror, merged[p]
+            )
+            row = (p + KSIZE - 1) * coil_share
+            lhs[local, row : row + coil_share] = jnp.where(
+                own_lane, merged[p] - mirror, crossed[p - 1]
+            )
+
+    def one(index, y, lhs, local):
+        real, imag = [
+            jnp.concatenate(
+                [maps_ref[y, index, part, pl.ds(first, coil_share)] for first in (own, other)],
+                axis=0,
+            )
+            for part in range(2)
+        ]
         filled = jnp.concatenate(
             [
                 jnp.concatenate([real, imag], axis=1),
@@ -294,7 +364,7 @@
         )
         halves = [filled, blank] if y == 0 else [blank, filled]
         mixed = jnp.dot(
-            rows_ref[index], jnp.concatenate(halves, axis=0), preferred_element_type=jnp.float32
+            lhs[local], jnp.concatenate(halves, axis=0), preferred_element_type=jnp.float32
         )
 
         def piece(place, part):
@@ -312,45 +382,49 @@
         result[y, index, 0] = out_real.astype(jnp.bfloat16)
         result[y, index, 1] = out_imag.astype(jnp.bfloat16)
 
-    def write(step, y):
-        span = pl.ds(step * SBLOCK, SBLOCK)
-        return pltpu.make_async_copy(result.at[y, span], out_ref.at[y, span], sems.at[step, y])
+    def write(step):
+        span = pl.ds(step * 2 * SBLOCK, 2 * SBLOCK)
+        return pltpu.make_async_copy(result.at[:, span], out_ref.at[:, span], sems.at[step])
 
     def block(step, carry):
-        for local in range(SBLOCK):
-            for y in range(2):
-                one(step * SBLOCK + local, y)
-        for y in range(2):
-            write(step, y).start()
+        first = step * 2 * SBLOCK
+        for current, following in ((0, 1), (1, 0)):
+            for local in range(SBLOCK):
+                index = first + current * SBLOCK + local
+                ahead = jnp.minimum(index + SBLOCK, slices - 1)
+                unpack(ahead, buffers[following], local)
+                for y in range(2):
+                    one(index, y, buffers[current], local)
+        write(step).start()
         return carry
 
-    steps = slices // SBLOCK
+    steps = slices // (2 * SBLOCK)
+    for local in range(SBLOCK):
+        unpack(local, buffers[0], local)
     lax.fori_loop(0, steps, block, 0)
-
-    def finish(step, carry):
-        for y in range(2):
-            write(step, y).wait()
-        return carry
-
-    lax.fori_loop(0, steps, finish, 0)
-
-
-def apply_rows(rows, maps):
+    for step in range(steps):
+        write(step).wait()
+
+
+def apply_rows(half, rows, maps):
     slices = rows.shape[0]
     width = maps.shape[0]
     shape = (width, slices, 2, COILS // 2, IMG)
     return pl.pallas_call(
         apply_kernel,
-        in_specs=[pl.BlockSpec(memory_space=pltpu.VMEM)] * 3,
+        in_specs=[pl.BlockSpec(memory_space=pltpu.SMEM)]
+        + [pl.BlockSpec(memory_space=pltpu.VMEM)] * 3,
         out_specs=pl.BlockSpec(memory_space=pltpu.HBM),
         out_shape=jax.ShapeDtypeStruct(shape, jnp.bfloat16),
         scratch_shapes=[
             pltpu.VMEM(shape, jnp.bfloat16),
-            pltpu.SemaphoreType.DMA((slices // SBLOCK, width)),
+            pltpu.VMEM((SBLOCK, SPAN * COILS // 2, LANES), jnp.bfloat16),
+            pltpu.VMEM((SBLOCK, SPAN * COILS // 2, LANES), jnp.bfloat16),
+            pltpu.SemaphoreType.DMA((slices // (2 * SBLOCK),)),
         ],
         compiler_params=pltpu.CompilerParams(vmem_limit_bytes=16 * 2**20),
         name="apply_rows",
-    )(rows, maps, jnp.asarray(phase_table()))
+    )(half, rows, maps, jnp.asarray(phase_table()))
 
 
 def shards(basis, picks, coil_maps):
@@ -359,7 +433,7 @@
     got = lax.ppermute(send, "col", [(0, 1), (1, 0)])
     rows = column_rows(half, keep, got)
     rows = lax.all_to_all(rows, "slc", split_axis=0, concat_axis=0, tiled=True)
-    return apply_rows(rows, coil_maps)
+    return apply_rows(half, rows, coil_maps)
 
 
 def solution(mesh):

time: 79.3 us -> 75.3 us (0.950)
  blocking collectives: 51.4 us -> 45.3 us
  Pallas kernels: 18.6 us -> 20.8 us
    all_to_all x1, blocking collectives: 51.4 us -> 45.3 us  [shards(): rows = lax.all_to_all(rows, 'slc', split_axis=0, concat_axis=0, tiled=True)]
    pallas_call x1, Pallas kernels: 5.03 us -> 6.54 us  [apply_rows(): pl.pallas_call(apply_kernel, in_specs=[pl.BlockSpec(memory_space=pltpu.SM...]
where the time goes in v1:
time: 75.3 us; the launch traced here: 75.2 us
  blocking collectives  45.3 us (60%)
  Pallas kernels  20.8 us (28%)
  waiting for transfers between devices  6.3 us (8%)
  starting transfers between devices  2.11 us (3%)
    all_to_all x1, blocking collectives, shards(): rows = lax.all_to_all(rows, 'slc', split_axis=0, concat_axis=0, tiled=True)  45.3 us
    pallas_call x1, Pallas kernels, partial_kernels(): pl.pallas_call(gram_kernel, in_specs=[pl.BlockSpec(memory_space=pltpu.VME...  9.87 us
    pallas_call x1, Pallas kernels, apply_rows(): pl.pallas_call(apply_kernel, in_specs=[pl.BlockSpec(memory_space=pltpu.SM...  6.54 us
    ppermute x1, waiting for transfers between devices, shards(): got = lax.ppermute(send, 'col', [(0, 1), (1, 0)])  6.3 us
    pallas_call x1, Pallas kernels, column_rows(): pl.pallas_call(transform_kernel, in_specs=[pl.BlockSpec(memory_space=pltp...  4.35 us
    ppermute x1, starting transfers between devices, shards(): got = lax.ppermute(send, 'col', [(0, 1), (1, 0)])  2.11 us
  transfers between devices with their start and end apart: 1, of which 1 were waited for; matrix products, arithmetic and copies ran while one was open for 0% of the time, Pallas kernels for 0%

profile of v1, /device:TPU:1, one launch (start us, length us, event | category | flops | bytes accessed | tf_op | source)
XLA Modules:
  0.0 75.2 jit_solution(17140642022209202108)
XLA Ops:
  0.0 0.0 copy-start.3
  0.0 0.7 copy-done.3
  0.7 0.0 copy-start.1
  0.7 9.9 %partial_kernels.1 = (f32[6,2,32,384]{3,2,1,0:T(8,128)S(1)}, bf16[6,2,32,384]{3,2,1,0:T(8,128)(2,1)S(1)}) custom-call(s32[1,304]{1,0:T(1,128)S(1)} %copy-done.3, bf16[2,1728,1152]{2,1,0:T(8,128)(2,1)} %bitcast.4), custom_call_target="tpu_custom_call" | custom-call | tf_op jit(solution)/shard_map/partial_kernels/pallas_call | solution.py:109
  10.6 2.1 %collective-permute-start = (bf16[6,2,32,384]{3,2,1,0:T(8,128)(2,1)S(1)}, bf16[6,2,32,384]{3,2,1,0:T(8,128)(2,1)S(1)}, u32[]{:S(2)}, u32[]{:S(2)}) collective-permute-start(bf16[6,2,32,384]{3,2,1,0:T(8,128)(2,1)S(1)} %get-tuple-element.8), channel_id=1, source_target_pairs={{0,1},{1,0},{2,3},{3,2},{4,5},{5,4},{6,7},{7,6},{8,9},{9,8},{10,11... | collective-permute-start | bytes 884744 | tf_op jit(solution)/shard_map/ppermute | solution.py:433
  12.7 6.3 %collective-permute-done.got_ref = bf16[6,2,32,384]{3,2,1,0:T(8,128)(2,1)S(1)} collective-permute-done((bf16[6,2,32,384]{3,2,1,0:T(8,128)(2,1)S(1)}, bf16[6,2,32,384]{3,2,1,0:T(8,128)(2,1)S(1)}, u32[]{:S(2)}, u32[]{:S(2)}) %collective-permute-start) | collective-permute-done | bytes 294944 | tf_op jit(solution)/shard_map/ppermute | solution.py:433
  19.0 0.0 copy-done.1
  19.0 4.3 %column_rows.1 = bf16[64,136,128]{2,1,0:T(8,128)(2,1)S(1)} custom-call(s32[1]{0:T(128)} %bitcast.half_ref, f32[6,2,32,384]{3,2,1,0:T(8,128)S(1)} %get-tuple-element.7.keep_ref, bf16[6,2,32,384]{3,2,1,0:T(8,128)(2,1)S(1)} %collective-permute-done.got_ref, f32[32,16,128]{2,1,0:T(8,128)S(1)} %copy-done.1), custom_call_target="tpu_custom_call" | custom-call | tf_op jit(solution)/shard_map/column_rows/pallas_call | solution.py:276
  23.3 0.0 copy-start
  23.3 0.0 copy-start.2
  23.4 45.3 %all_to_all.5.rows_ref = bf16[64,136,128]{2,1,0:T(8,128)(2,1)S(1)} all-to-all(bf16[64,136,128]{2,1,0:T(8,128)(2,1)S(1)} %column_rows.1), channel_id=1, replica_groups=mesh['slc'=64,'col'=2] {'slc'}, dimensions={0} | all-to-all | bytes 4456448 | tf_op jit(solution)/shard_map/all_to_all | solution.py:435
  68.6 0.0 copy-done
  68.6 0.0 copy-done.2
  68.6 6.5 %apply_rows.1 = bf16[2,64,2,16,128]{4,3,2,1,0:T(8,128)(2,1)} custom-call(s32[1]{0:T(128)} %bitcast.half_ref, bf16[64,136,128]{2,1,0:T(8,128)(2,1)S(1)} %all_to_all.5.rows_ref, bf16[2,64,2,32,128]{4,3,2,1,0:T(8,128)(2,1)S(1)} %copy-done, f32[16,128]{1,0:T(8,128)S(1)} %copy-done.2), custom_call_target="tpu_custom_call" | custom-call | tf_op jit(solution)/shard_map/apply_rows/pallas_call | solution.py:413
Async XLA Ops:
  0.0 0.7 copy-start.3
  0.7 18.3 %copy-start.1 = (f32[32,16,128]{2,1,0:T(8,128)S(1)}, f32[32,16,128]{2,1,0:T(8,128)}, u32[]{:S(2)}) copy-start(f32[32,16,128]{2,1,0:T(8,128)} %constant.8.clone.table_ref) | copy-start | bytes 786436
  10.6 8.4 %collective-permute-start = (bf16[6,2,32,384]{3,2,1,0:T(8,128)(2,1)S(1)}, bf16[6,2,32,384]{3,2,1,0:T(8,128)(2,1)S(1)}, u32[]{:S(2)}, u32[]{:S(2)}) collective-permute-start(bf16[6,2,32,384]{3,2,1,0:T(8,128)(2,1)S(1)} %get-tuple-element.8), channel_id=1, source_target_pairs={{0,1},{1,0},{2,3},{3,2},{4,5},{5,4},{6,7},{7,6},{8,9},{9,8},{10,11... | collective-permute-start | bytes 884744 | tf_op jit(solution)/shard_map/ppermute | solution.py:433
  23.3 45.3 %copy-start = (bf16[2,64,2,32,128]{4,3,2,1,0:T(8,128)(2,1)S(1)}, bf16[2,64,2,32,128]{4,3,2,1,0:T(8,128)(2,1)}, u32[]{:S(2)}) copy-start(bf16[2,64,2,32,128]{4,3,2,1,0:T(8,128)(2,1)} %maps_ref.1) | copy-start | bytes 6291460
  23.3 45.3 %copy-start.2 = (f32[16,128]{1,0:T(8,128)S(1)}, f32[16,128]{1,0:T(8,128)}, u32[]{:S(2)}) copy-start(f32[16,128]{1,0:T(8,128)} %constant.9.clone.table_ref) | copy-start | bytes 24580

commit v2 on v1

--- a/solution.py
+++ b/solution.py
@@ -16,16 +16,25 @@
 LANES = 128
 AROWS = KSIZE * COILS
 WIDE = 384
-SBLOCK = 4
+SBLOCK = 16
 PACKED = 136
+DEPTH = 2
 BF = jnp.bfloat16
 
 
-def gram_kernel(picks_ref, basis_ref, keep_ref, send_ref, buffer, onehot, rows, left, right, sems):
+def gram_kernel(
+    half_ref, picks_ref, basis_ref, keep_ref, send_ref,
+    chosen, buffer, onehot, picked, rows, left, right, pairs, sems, pick_sem,
+):
     windows = basis_ref.shape[1]
     width = basis_ref.shape[2]
     used = picks_ref.shape[1]
-    cuts = [(0, 512), (512, width - 512)]
+    coil_share = COILS // 2
+    own = pl.multiple_of(half_ref[0] * coil_share, coil_share)
+    other = pl.multiple_of(coil_share - half_ref[0] * coil_share, coil_share)
+    cuts = [(0, 256), (256, 384), (640, width - 640)]
+    fetch = pltpu.make_async_copy(picks_ref, chosen, pick_sem.at[0])
+    fetch.start()
     copies = [
         pltpu.make_async_copy(
             basis_ref.at[part, :, pl.ds(first, size)],
@@ -35,33 +44,30 @@
         for part in range(2)
         for index, (first, size) in enumerate(cuts)
     ]
-    for copy in copies:
+    for copy in copies[:DEPTH]:
         copy.start()
 
-    wanted = jnp.concatenate(
-        [picks_ref[...], jnp.full((1, WIDE - used), -1, jnp.int32)], axis=1
-    )
+    right[:, AROWS:, :] = jnp.zeros((2, right.shape[1] - AROWS, right.shape[2]), jnp.bfloat16)
+    for slot in range(2):
+        picked[slot, used:] = jnp.zeros((WIDE - used, picked.shape[2]), jnp.float32)
+    fetch.wait()
+    wanted = jnp.concatenate([chosen[...], jnp.full((1, WIDE - used), -1, jnp.int32)], axis=1)
     wanted = jnp.broadcast_to(wanted, (LANES, WIDE)).T[:used]
     lane = lax.broadcasted_iota(jnp.int32, (used, LANES), 1)
     for first in range(0, windows, LANES):
         size = min(LANES, windows - first)
         match = jnp.where(wanted == lane + first, 1.0, 0.0).astype(jnp.bfloat16)
         onehot[:, first : first + size] = match[:, :size]
-    right[:, AROWS:, :] = jnp.zeros((2, right.shape[1] - AROWS, right.shape[2]), jnp.bfloat16)
-
-    for part in range(2):
-        for index, (first, size) in enumerate(cuts):
-            copies[part * len(cuts) + index].wait()
-            picked = jnp.dot(
-                onehot[...],
-                buffer[part, :, first : first + size],
-                preferred_element_type=jnp.float32,
-            )
-            picked = jnp.concatenate([picked, jnp.zeros((WIDE - used, size), jnp.float32)], axis=0)
-            for tile in range(WIDE // LANES):
-                rows[part, tile, first : first + size] = picked[
-                    tile * LANES : (tile + 1) * LANES
-                ].T
+
+    def spread(position):
+        part, index = divmod(position, len(cuts))
+        first, size = cuts[index]
+        for tile in range(WIDE // LANES):
+            rows[part, tile, first : first + size] = picked[
+                position % 2, tile * LANES : (tile + 1) * LANES, :size
+            ].T
+        if index + 1 < len(cuts):
+            return
         for a in range(KSIZE):
             for b in range(KSIZE):
                 for tile in range(WIDE // LANES):
@@ -73,6 +79,21 @@
                     left[part, row, spot] = block
                     right[part, row, spot] = block
 
+    for position, copy in enumerate(copies):
+        part, index = divmod(position, len(cuts))
+        first, size = cuts[index]
+        copy.wait()
+        if position + DEPTH < len(copies):
+            copies[position + DEPTH].start()
+        picked[position % 2, :used, :size] = jnp.dot(
+            onehot[...],
+            buffer[part, :, first : first + size],
+            preferred_element_type=jnp.float32,
+        )
+        if position:
+            spread(position - 1)
+    spread(len(copies) - 1)
+
     def against(q, part):
         depth = (KSIZE - q) * WIDE
         lhs = left[:, :, :depth].reshape(2 * AROWS, depth)
@@ -84,50 +105,68 @@
         )
 
     pad = jnp.zeros((COILS, WIDE - right.shape[1]), jnp.float32)
-    for q in range(KSIZE):
-        with_real = against(q, 0)
-        with_imag = against(q, 1)
-        pair = (
-            with_real[:AROWS] + with_imag[AROWS:],
-            with_real[AROWS:] - with_imag[:AROWS],
-        )
+
+    def shift_sums(q):
         for part in range(2):
             total = None
             for a in range(KSIZE):
-                block = jnp.concatenate([pair[part][a * COILS : (a + 1) * COILS], pad], axis=1)
+                block = pairs[q % 2, part, a * COILS : (a + 1) * COILS]
+                block = jnp.concatenate([block, pad], axis=1)
                 shift = (KSIZE - 1 - a) * COILS
                 moved = pltpu.roll(block, shift, 1) if shift else block
                 total = moved if total is None else total + moved
             keep_ref[q, part] = total
-            send_ref[q, part] = total.astype(jnp.bfloat16)
-
-
-def partial_kernels(basis, picks):
+            send_ref[q, part] = keep_ref[q, part, pl.ds(other, coil_share)].astype(jnp.bfloat16)
+
+    for q in range(KSIZE):
+        with_real = against(q, 0)
+        with_imag = against(q, 1)
+        pairs[q % 2, 0] = with_real[:AROWS] + with_imag[AROWS:]
+        pairs[q % 2, 1] = with_real[AROWS:] - with_imag[:AROWS]
+        if q:
+            shift_sums(q - 1)
+    shift_sums(KSIZE - 1)
+    lane = lax.broadcasted_iota(jnp.int32, (coil_share, WIDE), 1)
+    theirs = lane // coil_share % 2 == 1 - half_ref[0]
+    toward = jnp.where(half_ref[0] == 0, WIDE - coil_share, coil_share)
+    for q in range(1, KSIZE, 2):
+        for part in range(2):
+            mixed = keep_ref[q, part, pl.ds(own, coil_share)]
+            if q + 1 < KSIZE:
+                extra = pltpu.roll(keep_ref[q + 1, part, pl.ds(own, coil_share)], toward, 1)
+                mixed = jnp.where(theirs, mixed, extra)
+            send_ref[KSIZE + q // 2, part] = mixed.astype(jnp.bfloat16)
+
+
+def partial_kernels(half, basis, picks):
     turned = pltpu.with_memory_space_constraint(jnp.transpose(basis, (0, 2, 1)), pltpu.HBM)
+    picks = pltpu.with_memory_space_constraint(picks, pltpu.HBM)
     parts, windows, rows = turned.shape
     used = picks.shape[1]
     return pl.pallas_call(
         gram_kernel,
-        in_specs=[
-            pl.BlockSpec(memory_space=pltpu.VMEM),
-            pl.BlockSpec(memory_space=pltpu.HBM),
-        ],
+        in_specs=[pl.BlockSpec(memory_space=pltpu.SMEM)]
+        + [pl.BlockSpec(memory_space=pltpu.HBM)] * 2,
         out_specs=[pl.BlockSpec(memory_space=pltpu.VMEM)] * 2,
         out_shape=[
             jax.ShapeDtypeStruct((KSIZE, 2, COILS, WIDE), jnp.float32),
-            jax.ShapeDtypeStruct((KSIZE, 2, COILS, WIDE), jnp.bfloat16),
+            jax.ShapeDtypeStruct((KSIZE + KSIZE // 2, 2, COILS // 2, WIDE), jnp.bfloat16),
         ],
         scratch_shapes=[
+            pltpu.VMEM((1, used), jnp.int32),
             pltpu.VMEM((parts, windows, rows), jnp.bfloat16),
             pltpu.VMEM((used, windows), jnp.bfloat16),
+            pltpu.VMEM((2, WIDE, 512), jnp.float32),
             pltpu.VMEM((parts, WIDE // LANES, rows, LANES), jnp.float32),
             pltpu.VMEM((2, AROWS, KSIZE * WIDE), jnp.bfloat16),
             pltpu.VMEM((2, 256, KSIZE * WIDE), jnp.bfloat16),
-            pltpu.SemaphoreType.DMA((parts, 2)),
+            pltpu.VMEM((2, 2, AROWS, 256), jnp.float32),
+            pltpu.SemaphoreType.DMA((parts, 3)),
+            pltpu.SemaphoreType.DMA((1,)),
         ],
-        compiler_params=pltpu.CompilerParams(vmem_limit_bytes=24 * 2**20),
+        compiler_params=pltpu.CompilerParams(vmem_limit_bytes=28 * 2**20),
         name="partial_kernels",
-    )(picks, turned)
+    )(half, picks, turned)
 
 
 def transform_table():
@@ -168,8 +207,8 @@
             found = []
             for tile in range(WIDE // LANES):
                 lanes = slice(tile * LANES, (tile + 1) * LANES)
-                real = own_first(whole[q, 0, pl.ds(own, coil_share), lanes])
-                imag = own_first(whole[q, 1, pl.ds(own, coil_share), lanes])
+                real = own_first(whole[q, 0, :, lanes])
+                imag = own_first(whole[q, 1, :, lanes])
                 first = jnp.where(even_slot, real, pltpu.roll(imag, COILS, 1))
                 second = jnp.where(even_slot, pltpu.roll(real, LANES - COILS, 1), imag)
                 first_turned = pltpu.roll(first, LANES // 2, 1)
@@ -202,17 +241,24 @@
             rest = coil_share // 2
             terms[index, row : row + rest] = jnp.where(own_lane[:rest], moved[rest:], gaps[4][:rest])
 
+        def own_sum(q, part):
+            mine = keep_ref[q, part, pl.ds(own, coil_share)]
+            return (mine + got_ref[q, part].astype(jnp.float32)) * factor
+
+        back = jnp.where(half_ref[0] == 0, WIDE - coil_share, coil_share)
+
+        def other_sum(q, part):
+            mine = keep_ref[q, part, pl.ds(other, coil_share)]
+            theirs = got_ref[KSIZE + (q - 1) // 2, part].astype(jnp.float32)
+            theirs = jnp.where(q % 2 == 1, theirs, pltpu.roll(theirs, back, 1))
+            return (mine + theirs) * factor
+
         def one_shift(q, carry):
-            real = (keep_ref[q, 0] + got_ref[q, 0].astype(jnp.float32)) * factor
-            imag = (keep_ref[q, 1] + got_ref[q, 1].astype(jnp.float32)) * factor
+            real = own_sum(q, 0)
+            imag = own_sum(q, 1)
             whole[q, 0] = real
             whole[q, 1] = imag
-            ordered = [
-                whole[q, part, pl.ds(first, coil_share), :]
-                for part in range(2)
-                for first in (own, other)
-            ]
-            ordered = [ordered[0], ordered[1], -ordered[2], -ordered[3]]
+            ordered = [real, other_sum(q, 0), -imag, -other_sum(q, 1)]
             turned[...] = jnp.concatenate(ordered + ordered, axis=0).T
             ahead = forward(q)
             sums = []
@@ -227,7 +273,7 @@
             return carry
 
         for part in range(2):
-            whole[0, part] = (keep_ref[0, part] + got_ref[0, part].astype(jnp.float32)) * factor
+            whole[0, part] = own_sum(0, part)
         place(0, forward(0))
         lax.fori_loop(1, KSIZE, one_shift, 0)
 
@@ -279,7 +325,7 @@
         + [pl.BlockSpec(memory_space=pltpu.VMEM)] * 3,
         out_specs=pl.BlockSpec(memory_space=pltpu.VMEM),
         scratch_shapes=[
-            pltpu.VMEM((KSIZE, 2, COILS, WIDE), jnp.float32),
+            pltpu.VMEM((KSIZE, 2, COILS // 2, WIDE), jnp.float32),
             pltpu.VMEM((WIDE, LANES), jnp.float32),
             pltpu.VMEM((2 * KSIZE - 1, PACKED, LANES), jnp.float32),
         ],
@@ -429,7 +475,7 @@
 
 def shards(basis, picks, coil_maps):
     half = lax.axis_index("col").astype(jnp.int32).reshape(1)
-    keep, send = partial_kernels(basis[0], picks)
+    keep, send = partial_kernels(half, basis[0], picks)
     got = lax.ppermute(send, "col", [(0, 1), (1, 0)])
     rows = column_rows(half, keep, got)
     rows = lax.all_to_all(rows, "slc", split_axis=0, concat_axis=0, tiled=True)

time: 75.3 us -> 71.4 us (0.948)
  Pallas kernels: 20.8 us -> 19.1 us
  waiting for transfers between devices: 6.3 us -> 4.7 us
    ppermute x1, waiting for transfers between devices: 6.3 us -> 4.7 us  [shards(): got = lax.ppermute(send, 'col', [(0, 1), (1, 0)])]
    pallas_call x1, Pallas kernels: 6.54 us -> 5.01 us  [apply_rows(): pl.pallas_call(apply_kernel, in_specs=[pl.BlockSpec(memory_space=pltpu.SM...]
where the time goes in v2:
time: 71.4 us; the launch traced here: 71.2 us
  blocking collectives  45.3 us (63%)
  Pallas kernels  19.1 us (27%)
  waiting for transfers between devices  4.7 us (7%)
  starting transfers between devices  2.09 us (3%)
    all_to_all x1, blocking collectives, shards(): rows = lax.all_to_all(rows, 'slc', split_axis=0, concat_axis=0, tiled=True)  45.3 us
    pallas_call x1, Pallas kernels, partial_kernels(): pl.pallas_call(gram_kernel, in_specs=[pl.BlockSpec(memory_space=pltpu.SME...  9.98 us
    pallas_call x1, Pallas kernels, apply_rows(): pl.pallas_call(apply_kernel, in_specs=[pl.BlockSpec(memory_space=pltpu.SM...  5.01 us
    ppermute x1, waiting for transfers between devices, shards(): got = lax.ppermute(send, 'col', [(0, 1), (1, 0)])  4.7 us
    pallas_call x1, Pallas kernels, column_rows(): pl.pallas_call(transform_kernel, in_specs=[pl.BlockSpec(memory_space=pltp...  4.07 us
    ppermute x1, starting transfers between devices, shards(): got = lax.ppermute(send, 'col', [(0, 1), (1, 0)])  2.09 us
  transfers between devices with their start and end apart: 1, of which 1 were waited for; matrix products, arithmetic and copies ran while one was open for 0% of the time, Pallas kernels for 0%

profile of v2, /device:TPU:1, one launch (start us, length us, event | category | flops | bytes accessed | tf_op | source)
XLA Modules:
  0.0 71.2 jit_solution(10638314400327284812)
XLA Ops:
  0.0 0.0 copy-start.1
  0.0 10.0 %partial_kernels.1 = (f32[6,2,32,384]{3,2,1,0:T(8,128)S(1)}, bf16[9,2,16,384]{3,2,1,0:T(8,128)(2,1)S(1)}) custom-call(s32[1]{0:T(128)} %bitcast.half_ref, s32[1,304]{1,0:T(1,128)} %picks_ref.1, bf16[2,1728,1152]{2,1,0:T(8,128)(2,1)} %bitcast.4), custom_call_target="tpu_custom_call" | custom-call | tf_op jit(solution)/shard_map/partial_kernels/pallas_call | solution.py:146
  10.0 2.1 %collective-permute-start = (bf16[9,2,16,384]{3,2,1,0:T(8,128)(2,1)S(1)}, bf16[9,2,16,384]{3,2,1,0:T(8,128)(2,1)S(1)}, u32[]{:S(2)}, u32[]{:S(2)}) collective-permute-start(bf16[9,2,16,384]{3,2,1,0:T(8,128)(2,1)S(1)} %get-tuple-element.8), channel_id=1, source_target_pairs={{0,1},{1,0},{2,3},{3,2},{4,5},{5,4},{6,7},{7,6},{8,9},{9,8},{10,11... | collective-permute-start | bytes 663560 | tf_op jit(solution)/shard_map/ppermute | solution.py:479
  12.1 4.7 %collective-permute-done.got_ref = bf16[9,2,16,384]{3,2,1,0:T(8,128)(2,1)S(1)} collective-permute-done((bf16[9,2,16,384]{3,2,1,0:T(8,128)(2,1)S(1)}, bf16[9,2,16,384]{3,2,1,0:T(8,128)(2,1)S(1)}, u32[]{:S(2)}, u32[]{:S(2)}) %collective-permute-start) | collective-permute-done | bytes 221216 | tf_op jit(solution)/shard_map/ppermute | solution.py:479
  16.8 0.0 copy-done.1
  16.8 4.1 %column_rows.1 = bf16[64,136,128]{2,1,0:T(8,128)(2,1)S(1)} custom-call(s32[1]{0:T(128)} %bitcast.half_ref, f32[6,2,32,384]{3,2,1,0:T(8,128)S(1)} %get-tuple-element.7.keep_ref, bf16[9,2,16,384]{3,2,1,0:T(8,128)(2,1)S(1)} %collective-permute-done.got_ref, f32[32,16,128]{2,1,0:T(8,128)S(1)} %copy-done.1), custom_call_target="tpu_custom_call" | custom-call | tf_op jit(solution)/shard_map/column_rows/pallas_call | solution.py:322
  20.9 0.0 copy-start
  20.9 0.0 copy-start.2
  20.9 45.3 %all_to_all.5.rows_ref = bf16[64,136,128]{2,1,0:T(8,128)(2,1)S(1)} all-to-all(bf16[64,136,128]{2,1,0:T(8,128)(2,1)S(1)} %column_rows.1), channel_id=1, replica_groups=mesh['slc'=64,'col'=2] {'slc'}, dimensions={0} | all-to-all | bytes 4456448 | tf_op jit(solution)/shard_map/all_to_all | solution.py:481
  66.2 0.0 copy-done
  66.2 0.0 copy-done.2
  66.2 5.0 %apply_rows.1 = bf16[2,64,2,16,128]{4,3,2,1,0:T(8,128)(2,1)} custom-call(s32[1]{0:T(128)} %bitcast.half_ref, bf16[64,136,128]{2,1,0:T(8,128)(2,1)S(1)} %all_to_all.5.rows_ref, bf16[2,64,2,32,128]{4,3,2,1,0:T(8,128)(2,1)S(1)} %copy-done, f32[16,128]{1,0:T(8,128)S(1)} %copy-done.2), custom_call_target="tpu_custom_call" | custom-call | tf_op jit(solution)/shard_map/apply_rows/pallas_call | solution.py:459
Async XLA Ops:
  0.0 16.8 %copy-start.1 = (f32[32,16,128]{2,1,0:T(8,128)S(1)}, f32[32,16,128]{2,1,0:T(8,128)}, u32[]{:S(2)}) copy-start(f32[32,16,128]{2,1,0:T(8,128)} %constant.8.clone.table_ref) | copy-start | bytes 786436
  10.0 6.8 %collective-permute-start = (bf16[9,2,16,384]{3,2,1,0:T(8,128)(2,1)S(1)}, bf16[9,2,16,384]{3,2,1,0:T(8,128)(2,1)S(1)}, u32[]{:S(2)}, u32[]{:S(2)}) collective-permute-start(bf16[9,2,16,384]{3,2,1,0:T(8,128)(2,1)S(1)} %get-tuple-element.8), channel_id=1, source_target_pairs={{0,1},{1,0},{2,3},{3,2},{4,5},{5,4},{6,7},{7,6},{8,9},{9,8},{10,11... | collective-permute-start | bytes 663560 | tf_op jit(solution)/shard_map/ppermute | solution.py:479
  20.9 45.3 %copy-start = (bf16[2,64,2,32,128]{4,3,2,1,0:T(8,128)(2,1)S(1)}, bf16[2,64,2,32,128]{4,3,2,1,0:T(8,128)(2,1)}, u32[]{:S(2)}) copy-start(bf16[2,64,2,32,128]{4,3,2,1,0:T(8,128)(2,1)} %maps_ref.1) | copy-start | bytes 6291460
  20.9 45.3 %copy-start.2 = (f32[16,128]{1,0:T(8,128)S(1)}, f32[16,128]{1,0:T(8,128)}, u32[]{:S(2)}) copy-start(f32[16,128]{1,0:T(8,128)} %constant.9.clone.table_ref) | copy-start | bytes 24580

commit v3 on v2

--- a/solution.py
+++ b/solution.py
@@ -32,7 +32,7 @@
     coil_share = COILS // 2
     own = pl.multiple_of(half_ref[0] * coil_share, coil_share)
     other = pl.multiple_of(coil_share - half_ref[0] * coil_share, coil_share)
-    cuts = [(0, 256), (256, 384), (640, width - 640)]
+    cuts = [(0, 512), (512, width - 512)]
     fetch = pltpu.make_async_copy(picks_ref, chosen, pick_sem.at[0])
     fetch.start()
     copies = [
@@ -156,7 +156,7 @@
             pltpu.VMEM((1, used), jnp.int32),
             pltpu.VMEM((parts, windows, rows), jnp.bfloat16),
             pltpu.VMEM((used, windows), jnp.bfloat16),
-            pltpu.VMEM((2, WIDE, 512), jnp.float32),
+            pltpu.VMEM((2, WIDE, 640), jnp.float32),
             pltpu.VMEM((parts, WIDE // LANES, rows, LANES), jnp.float32),
             pltpu.VMEM((2, AROWS, KSIZE * WIDE), jnp.bfloat16),
             pltpu.VMEM((2, 256, KSIZE * WIDE), jnp.bfloat16),

time: 71.4 us -> 71 us (level)
  no operation moved by 1% of the time
where the time goes in v3:
time: 71 us; the launch traced here: 70.9 us
  blocking collectives  45.3 us (64%)
  Pallas kernels  18.7 us (26%)
  waiting for transfers between devices  4.71 us (7%)
  starting transfers between devices  2.1 us (3%)
    all_to_all x1, blocking collectives, shards(): rows = lax.all_to_all(rows, 'slc', split_axis=0, concat_axis=0, tiled=True)  45.3 us
    pallas_call x1, Pallas kernels, partial_kernels(): pl.pallas_call(gram_kernel, in_specs=[pl.BlockSpec(memory_space=pltpu.SME...  9.65 us
    pallas_call x1, Pallas kernels, apply_rows(): pl.pallas_call(apply_kernel, in_specs=[pl.BlockSpec(memory_space=pltpu.SM...  5 us
    ppermute x1, waiting for transfers between devices, shards(): got = lax.ppermute(send, 'col', [(0, 1), (1, 0)])  4.71 us
    pallas_call x1, Pallas kernels, column_rows(): pl.pallas_call(transform_kernel, in_specs=[pl.BlockSpec(memory_space=pltp...  4.07 us
    ppermute x1, starting transfers between devices, shards(): got = lax.ppermute(send, 'col', [(0, 1), (1, 0)])  2.1 us
  transfers between devices with their start and end apart: 1, of which 1 were waited for; matrix products, arithmetic and copies ran while one was open for 0% of the time, Pallas kernels for 0%

profile of v3, /device:TPU:1, one launch (start us, length us, event | category | flops | bytes accessed | tf_op | source)
XLA Modules:
  0.0 70.9 jit_solution(13304863449478869332)
XLA Ops:
  0.0 0.0 copy-start.1
  0.0 9.7 %partial_kernels.1 = (f32[6,2,32,384]{3,2,1,0:T(8,128)S(1)}, bf16[9,2,16,384]{3,2,1,0:T(8,128)(2,1)S(1)}) custom-call(s32[1]{0:T(128)} %bitcast.half_ref, s32[1,304]{1,0:T(1,128)} %picks_ref.1, bf16[2,1728,1152]{2,1,0:T(8,128)(2,1)} %bitcast.4), custom_call_target="tpu_custom_call" | custom-call | tf_op jit(solution)/shard_map/partial_kernels/pallas_call | solution.py:146
  9.7 2.1 %collective-permute-start = (bf16[9,2,16,384]{3,2,1,0:T(8,128)(2,1)S(1)}, bf16[9,2,16,384]{3,2,1,0:T(8,128)(2,1)S(1)}, u32[]{:S(2)}, u32[]{:S(2)}) collective-permute-start(bf16[9,2,16,384]{3,2,1,0:T(8,128)(2,1)S(1)} %get-tuple-element.8), channel_id=1, source_target_pairs={{0,1},{1,0},{2,3},{3,2},{4,5},{5,4},{6,7},{7,6},{8,9},{9,8},{10,11... | collective-permute-start | bytes 663560 | tf_op jit(solution)/shard_map/ppermute | solution.py:479
  11.8 4.7 %collective-permute-done.got_ref = bf16[9,2,16,384]{3,2,1,0:T(8,128)(2,1)S(1)} collective-permute-done((bf16[9,2,16,384]{3,2,1,0:T(8,128)(2,1)S(1)}, bf16[9,2,16,384]{3,2,1,0:T(8,128)(2,1)S(1)}, u32[]{:S(2)}, u32[]{:S(2)}) %collective-permute-start) | collective-permute-done | bytes 221216 | tf_op jit(solution)/shard_map/ppermute | solution.py:479
  16.5 0.0 copy-done.1
  16.5 4.1 %column_rows.1 = bf16[64,136,128]{2,1,0:T(8,128)(2,1)S(1)} custom-call(s32[1]{0:T(128)} %bitcast.half_ref, f32[6,2,32,384]{3,2,1,0:T(8,128)S(1)} %get-tuple-element.7.keep_ref, bf16[9,2,16,384]{3,2,1,0:T(8,128)(2,1)S(1)} %collective-permute-done.got_ref, f32[32,16,128]{2,1,0:T(8,128)S(1)} %copy-done.1), custom_call_target="tpu_custom_call" | custom-call | tf_op jit(solution)/shard_map/column_rows/pallas_call | solution.py:322
  20.6 0.0 copy-start
  20.6 0.0 copy-start.2
  20.6 45.3 %all_to_all.5.rows_ref = bf16[64,136,128]{2,1,0:T(8,128)(2,1)S(1)} all-to-all(bf16[64,136,128]{2,1,0:T(8,128)(2,1)S(1)} %column_rows.1), channel_id=1, replica_groups=mesh['slc'=64,'col'=2] {'slc'}, dimensions={0} | all-to-all | bytes 4456448 | tf_op jit(solution)/shard_map/all_to_all | solution.py:481
  65.9 0.0 copy-done
  65.9 0.0 copy-done.2
  65.9 5.0 %apply_rows.1 = bf16[2,64,2,16,128]{4,3,2,1,0:T(8,128)(2,1)} custom-call(s32[1]{0:T(128)} %bitcast.half_ref, bf16[64,136,128]{2,1,0:T(8,128)(2,1)S(1)} %all_to_all.5.rows_ref, bf16[2,64,2,32,128]{4,3,2,1,0:T(8,128)(2,1)S(1)} %copy-done, f32[16,128]{1,0:T(8,128)S(1)} %copy-done.2), custom_call_target="tpu_custom_call" | custom-call | tf_op jit(solution)/shard_map/apply_rows/pallas_call | solution.py:459
Async XLA Ops:
  0.0 16.5 %copy-start.1 = (f32[32,16,128]{2,1,0:T(8,128)S(1)}, f32[32,16,128]{2,1,0:T(8,128)}, u32[]{:S(2)}) copy-start(f32[32,16,128]{2,1,0:T(8,128)} %constant.8.clone.table_ref) | copy-start | bytes 786436
  9.7 6.8 %collective-permute-start = (bf16[9,2,16,384]{3,2,1,0:T(8,128)(2,1)S(1)}, bf16[9,2,16,384]{3,2,1,0:T(8,128)(2,1)S(1)}, u32[]{:S(2)}, u32[]{:S(2)}) collective-permute-start(bf16[9,2,16,384]{3,2,1,0:T(8,128)(2,1)S(1)} %get-tuple-element.8), channel_id=1, source_target_pairs={{0,1},{1,0},{2,3},{3,2},{4,5},{5,4},{6,7},{7,6},{8,9},{9,8},{10,11... | collective-permute-start | bytes 663560 | tf_op jit(solution)/shard_map/ppermute | solution.py:479
  20.6 45.3 %copy-start = (bf16[2,64,2,32,128]{4,3,2,1,0:T(8,128)(2,1)S(1)}, bf16[2,64,2,32,128]{4,3,2,1,0:T(8,128)(2,1)}, u32[]{:S(2)}) copy-start(bf16[2,64,2,32,128]{4,3,2,1,0:T(8,128)(2,1)} %maps_ref.1) | copy-start | bytes 6291460
  20.6 45.3 %copy-start.2 = (f32[16,128]{1,0:T(8,128)S(1)}, f32[16,128]{1,0:T(8,128)}, u32[]{:S(2)}) copy-start(f32[16,128]{1,0:T(8,128)} %constant.9.clone.table_ref) | copy-start | bytes 24580

commit v4 on v3

--- a/solution.py
+++ b/solution.py
@@ -279,7 +279,7 @@
 
     build()
     blocks = table_ref.shape[0]
-    group_size = 2
+    group_size = 4
 
     def one(step, carry):
         places = [step * group_size + extra for extra in range(group_size)]

time: 71 us -> 71 us (level)
  no operation moved by 1% of the time
where the time goes in v4:
time: 71 us; the launch traced here: 70.8 us
  blocking collectives  45.3 us (64%)
  Pallas kernels  18.7 us (26%)
  waiting for transfers between devices  4.71 us (7%)
  starting transfers between devices  2.1 us (3%)
    all_to_all x1, blocking collectives, shards(): rows = lax.all_to_all(rows, 'slc', split_axis=0, concat_axis=0, tiled=True)  45.3 us
    pallas_call x1, Pallas kernels, partial_kernels(): pl.pallas_call(gram_kernel, in_specs=[pl.BlockSpec(memory_space=pltpu.SME...  9.65 us
    pallas_call x1, Pallas kernels, apply_rows(): pl.pallas_call(apply_kernel, in_specs=[pl.BlockSpec(memory_space=pltpu.SM...  5.01 us
    ppermute x1, waiting for transfers between devices, shards(): got = lax.ppermute(send, 'col', [(0, 1), (1, 0)])  4.71 us
    pallas_call x1, Pallas kernels, column_rows(): pl.pallas_call(transform_kernel, in_specs=[pl.BlockSpec(memory_space=pltp...  4.03 us
    ppermute x1, starting transfers between devices, shards(): got = lax.ppermute(send, 'col', [(0, 1), (1, 0)])  2.1 us
  transfers between devices with their start and end apart: 1, of which 1 were waited for; matrix products, arithmetic and copies ran while one was open for 0% of the time, Pallas kernels for 0%

profile of v4, /device:TPU:1, one launch (start us, length us, event | category | flops | bytes accessed | tf_op | source)
XLA Modules:
  0.0 70.8 jit_solution(4756928946010842059)
XLA Ops:
  0.0 0.0 copy-start.1
  0.0 9.7 %partial_kernels.1 = (f32[6,2,32,384]{3,2,1,0:T(8,128)S(1)}, bf16[9,2,16,384]{3,2,1,0:T(8,128)(2,1)S(1)}) custom-call(s32[1]{0:T(128)} %bitcast.half_ref, s32[1,304]{1,0:T(1,128)} %picks_ref.1, bf16[2,1728,1152]{2,1,0:T(8,128)(2,1)} %bitcast.4), custom_call_target="tpu_custom_call" | custom-call | tf_op jit(solution)/shard_map/partial_kernels/pallas_call | solution.py:146
  9.7 2.1 %collective-permute-start = (bf16[9,2,16,384]{3,2,1,0:T(8,128)(2,1)S(1)}, bf16[9,2,16,384]{3,2,1,0:T(8,128)(2,1)S(1)}, u32[]{:S(2)}, u32[]{:S(2)}) collective-permute-start(bf16[9,2,16,384]{3,2,1,0:T(8,128)(2,1)S(1)} %get-tuple-element.8), channel_id=1, source_target_pairs={{0,1},{1,0},{2,3},{3,2},{4,5},{5,4},{6,7},{7,6},{8,9},{9,8},{10,11... | collective-permute-start | bytes 663560 | tf_op jit(solution)/shard_map/ppermute | solution.py:479
  11.8 4.7 %collective-permute-done.got_ref = bf16[9,2,16,384]{3,2,1,0:T(8,128)(2,1)S(1)} collective-permute-done((bf16[9,2,16,384]{3,2,1,0:T(8,128)(2,1)S(1)}, bf16[9,2,16,384]{3,2,1,0:T(8,128)(2,1)S(1)}, u32[]{:S(2)}, u32[]{:S(2)}) %collective-permute-start) | collective-permute-done | bytes 221216 | tf_op jit(solution)/shard_map/ppermute | solution.py:479
  16.5 0.0 copy-done.1
  16.5 4.0 %column_rows.1 = bf16[64,136,128]{2,1,0:T(8,128)(2,1)S(1)} custom-call(s32[1]{0:T(128)} %bitcast.half_ref, f32[6,2,32,384]{3,2,1,0:T(8,128)S(1)} %get-tuple-element.7.keep_ref, bf16[9,2,16,384]{3,2,1,0:T(8,128)(2,1)S(1)} %collective-permute-done.got_ref, f32[32,16,128]{2,1,0:T(8,128)S(1)} %copy-done.1), custom_call_target="tpu_custom_call" | custom-call | tf_op jit(solution)/shard_map/column_rows/pallas_call | solution.py:322
  20.5 0.0 copy-start
  20.5 0.0 copy-start.2
  20.5 45.3 %all_to_all.5.rows_ref = bf16[64,136,128]{2,1,0:T(8,128)(2,1)S(1)} all-to-all(bf16[64,136,128]{2,1,0:T(8,128)(2,1)S(1)} %column_rows.1), channel_id=1, replica_groups=mesh['slc'=64,'col'=2] {'slc'}, dimensions={0} | all-to-all | bytes 4456448 | tf_op jit(solution)/shard_map/all_to_all | solution.py:481
  65.8 0.0 copy-done
  65.8 0.0 copy-done.2
  65.8 5.0 %apply_rows.1 = bf16[2,64,2,16,128]{4,3,2,1,0:T(8,128)(2,1)} custom-call(s32[1]{0:T(128)} %bitcast.half_ref, bf16[64,136,128]{2,1,0:T(8,128)(2,1)S(1)} %all_to_all.5.rows_ref, bf16[2,64,2,32,128]{4,3,2,1,0:T(8,128)(2,1)S(1)} %copy-done, f32[16,128]{1,0:T(8,128)S(1)} %copy-done.2), custom_call_target="tpu_custom_call" | custom-call | tf_op jit(solution)/shard_map/apply_rows/pallas_call | solution.py:459
Async XLA Ops:
  0.0 16.5 %copy-start.1 = (f32[32,16,128]{2,1,0:T(8,128)S(1)}, f32[32,16,128]{2,1,0:T(8,128)}, u32[]{:S(2)}) copy-start(f32[32,16,128]{2,1,0:T(8,128)} %constant.8.clone.table_ref) | copy-start | bytes 786436
  9.7 6.8 %collective-permute-start = (bf16[9,2,16,384]{3,2,1,0:T(8,128)(2,1)S(1)}, bf16[9,2,16,384]{3,2,1,0:T(8,128)(2,1)S(1)}, u32[]{:S(2)}, u32[]{:S(2)}) collective-permute-start(bf16[9,2,16,384]{3,2,1,0:T(8,128)(2,1)S(1)} %get-tuple-element.8), channel_id=1, source_target_pairs={{0,1},{1,0},{2,3},{3,2},{4,5},{5,4},{6,7},{7,6},{8,9},{9,8},{10,11... | collective-permute-start | bytes 663560 | tf_op jit(solution)/shard_map/ppermute | solution.py:479
  20.5 45.3 %copy-start = (bf16[2,64,2,32,128]{4,3,2,1,0:T(8,128)(2,1)S(1)}, bf16[2,64,2,32,128]{4,3,2,1,0:T(8,128)(2,1)}, u32[]{:S(2)}) copy-start(bf16[2,64,2,32,128]{4,3,2,1,0:T(8,128)(2,1)} %maps_ref.1) | copy-start | bytes 6291460
  20.5 45.3 %copy-start.2 = (f32[16,128]{1,0:T(8,128)S(1)}, f32[16,128]{1,0:T(8,128)}, u32[]{:S(2)}) copy-start(f32[16,128]{1,0:T(8,128)} %constant.9.clone.table_ref) | copy-start | bytes 24580
